TPU v7x, 32 devices: a whole 2x2x4 slice. The times are simulated.
32 devices in a mesh: ctg: 8 (over y, x, core), br: 4 (over z).
Axes of the slice: x: 2, y: 2, z: 4, core: 2. Of those that a mesh axis runs over, the one named last changes fastest.
Arguments:
- base_vm: float32 [10240], P(('ctg', 'br')), may hold values from 0.95 to 1.05
- base_va: float32 [10240], P(('ctg', 'br')), may hold values from -0.6 to 0.6
- delta_state: float32 [64, 2, 10240], P('ctg', None, 'br'), may hold values from -0.18 to 0.18
- multipliers: float32 [64, 2, 10240], P('ctg', None, 'br'), may hold values from -6 to 6
- net_inj: float32 [64, 2, 10240], P('ctg', None, 'br'), may hold values from -6 to 6
- ang_grad: float32 [64, 10240], P('ctg', 'br'), may hold values from -6 to 6
- from_bus: int32 [13312], P('br'), may hold values from 0 to 10239
- to_bus: int32 [13312], P('br'), may hold values from 0 to 10239
- status: int32 [64, 13312], P('ctg', 'br'), may hold values 0 or 1
- conduct: float32 [13312], P('br'), may hold values from 1 to 5
- suscept: float32 [13312], P('br'), may hold values from -15 to -5
- charging: float32 [13312], P('br'), may hold values from 0.1 to 0.6
- rating: float32 [13312], P('br'), may hold values from 1 to 3
- slack: float32 [64, 13312], P('ctg', 'br'), may hold values from 0.05 to 2
- zdual: float32 [64, 13312], P('ctg', 'br'), may hold values from 0.05 to 2
Outputs:
- mismatch: float32 [64, 2, 10240], P('ctg', None, 'br')
- dual_res: float32 [64, 10240], P('ctg', 'br')
- limit_res: float32 [64, 13312], P('ctg', 'br')
- ctg_norms: float32 [64, 4], P('ctg')
- total_norms: float32 [4], replicated
All inputs are finite; a program needn't handle non-finite values. No bound on the sum of `status` on one device may be relied on, other than what follows from the above.
Results may differ from a plain program's by a relative error of at most 0.0003.
Values sent between devices are 32-bit elements; how exact they have to be, the bound alone decides.
A program may use at most 64 MiB of HBM per device.

v0:
```python
import math
import jax
import jax.numpy as jnp
from jax import lax
from jax.sharding import PartitionSpec as P


def block_size(span_total, other_side):
    limit = max(128, (1 << 23) // other_side)
    power = 1 << limit.bit_length() - 1
    return math.gcd(span_total, min(1024, power))


def select_cols(values, index_list):
    row_count, bus_count = values.shape
    col_count = index_list.shape[0]
    span_cols = block_size(bus_count, col_count)
    block_count = bus_count // span_cols
    tiles = values.reshape(row_count, block_count, span_cols).transpose(1, 0, 2)

    def add_block(running, item):
        segment, number = item
        labels = number * span_cols + lax.iota(jnp.int32, span_cols)
        onehot = (labels[:, None] == index_list[None, :]).astype(jnp.float32)
        running = running + jnp.dot(
            segment, onehot, precision=lax.Precision.HIGHEST, preferred_element_type=jnp.float32
        )
        return (running, None)

    start_zero = jnp.zeros((row_count, col_count), jnp.float32)
    numbers = jnp.arange(block_count, dtype=jnp.int32)
    result, _ = lax.scan(add_block, start_zero, (tiles, numbers))
    return result


def spread_rows(values, index_list, bus_count):
    row_count, col_count = values.shape
    span_cols = block_size(bus_count, col_count)
    block_count = bus_count // span_cols

    def one_block(carry, number):
        labels = number * span_cols + lax.iota(jnp.int32, span_cols)
        onehot = (index_list[:, None] == labels[None, :]).astype(jnp.float32)
        piece_sum = jnp.dot(
            values, onehot, precision=lax.Precision.HIGHEST, preferred_element_type=jnp.float32
        )
        return (carry, piece_sum)

    numbers = jnp.arange(block_count, dtype=jnp.int32)
    _, pieces = lax.scan(one_block, jnp.int32(0), numbers)
    return pieces.transpose(1, 0, 2).reshape(row_count, bus_count)


def branch_flows(
    volt_mag, volt_ang, mult_p, mult_q, from_idx, to_idx, conduct, suscept, charging, in_service
):
    scen_count = volt_mag.shape[0]
    stacked = jnp.concatenate([volt_mag, volt_ang, mult_p, mult_q], 0)
    at_from_end = select_cols(stacked, from_idx)
    at_to_end = select_cols(stacked, to_idx)
    volt_from = at_from_end[:scen_count]
    volt_to = at_to_end[:scen_count]
    angle_diff = at_from_end[scen_count : 2 * scen_count] - at_to_end[scen_count : 2 * scen_count]
    mp_from = at_from_end[2 * scen_count : 3 * scen_count]
    mq_from = at_from_end[3 * scen_count :]
    mp_to = at_to_end[2 * scen_count : 3 * scen_count]
    mq_to = at_to_end[3 * scen_count :]
    cos_diff = jnp.cos(angle_diff)
    sin_diff = jnp.sin(angle_diff)
    volt_prod = volt_from * volt_to
    p_from = conduct * volt_from * volt_from - volt_prod * (conduct * cos_diff + suscept * sin_diff)
    q_from = -(suscept + charging) * volt_from * volt_from - volt_prod * (
        conduct * sin_diff - suscept * cos_diff
    )
    p_to = conduct * volt_to * volt_to - volt_prod * (conduct * cos_diff - suscept * sin_diff)
    q_to = -(suscept + charging) * volt_to * volt_to + volt_prod * (
        conduct * sin_diff + suscept * cos_diff
    )
    flow_dual = volt_prod * (
        mp_from * (conduct * sin_diff - suscept * cos_diff)
        - mq_from * (conduct * cos_diff + suscept * sin_diff)
        + mp_to * (conduct * sin_diff + suscept * cos_diff)
        + mq_to * (conduct * cos_diff - suscept * sin_diff)
    )
    at_from = jnp.stack([p_from, q_from, flow_dual], 1) * in_service[:, None, :]
    at_to = jnp.stack([p_to, q_to, -flow_dual], 1) * in_service[:, None, :]
    return (at_from, at_to)


def sum_at_buses(from_vals, to_vals, from_idx, to_idx, offset, bus_count):
    scen_count = from_vals.shape[0]
    both_vals = jnp.concatenate([from_vals, to_vals], 2).reshape(scen_count * 3, -1)
    both_idx = jnp.concatenate([from_idx, to_idx], 0) - offset
    summed = spread_rows(both_vals, both_idx, bus_count)
    return summed.reshape(scen_count, 3, bus_count)


def per_device(
    base_vm,
    base_va,
    delta_state,
    multipliers,
    net_inj,
    ang_grad,
    from_bus,
    to_bus,
    status,
    conduct,
    suscept,
    charging,
    rating,
    slack,
    zdual,
):
    full_vm, full_va = (
        lax.all_gather(base_vm, ("ctg", "br"), axis=0, tiled=True),
        lax.all_gather(base_va, ("ctg", "br"), axis=0, tiled=True),
    )
    shifts, duals_all = (
        lax.all_gather(delta_state, "br", axis=2, tiled=True),
        lax.all_gather(multipliers, "br", axis=2, tiled=True),
    )
    volt_mag = full_vm[None, :] + shifts[:, 0]
    volt_ang = full_va[None, :] + shifts[:, 1]
    own_buses = delta_state.shape[2]
    offset = lax.axis_index("br") * own_buses
    in_service = status.astype(jnp.float32)
    at_from, at_to = branch_flows(
        volt_mag,
        volt_ang,
        duals_all[:, 0],
        duals_all[:, 1],
        from_bus,
        to_bus,
        conduct,
        suscept,
        charging,
        in_service,
    )
    limit_res = in_service * (
        at_from[:, 0] * at_from[:, 0] + at_from[:, 1] * at_from[:, 1] + slack - rating * rating
    )
    complement = in_service * (zdual * slack - 0.01)
    limit_part = jnp.sum(limit_res * limit_res, axis=1)
    comp_part = jnp.sum(complement * complement, axis=1)
    limit_sq, comp_sq = lax.psum((limit_part, comp_part), "br")
    every_from, every_to = (
        lax.all_gather(at_from, "br", axis=2, tiled=True),
        lax.all_gather(at_to, "br", axis=2, tiled=True),
    )
    ends_from, ends_to = (
        lax.all_gather(from_bus, "br", axis=0, tiled=True),
        lax.all_gather(to_bus, "br", axis=0, tiled=True),
    )
    summed = sum_at_buses(every_from, every_to, ends_from, ends_to, offset, own_buses)
    mismatch = summed[:, :2] - net_inj
    dual_res = summed[:, 2] + ang_grad
    mis_part = jnp.sum(mismatch * mismatch, axis=(1, 2))
    dual_part = jnp.sum(dual_res * dual_res, axis=1)
    mis_sq, dual_sq = lax.psum((mis_part, dual_part), "br")
    squares = jnp.stack([mis_sq, dual_sq, limit_sq, comp_sq], 1)
    ctg_norms = jnp.sqrt(squares)
    totals = lax.psum(jnp.sum(squares, axis=0), "ctg")
    total_norms = jnp.sqrt(totals / (delta_state.shape[0] * lax.axis_size("ctg")))
    return (mismatch, dual_res, limit_res, ctg_norms, total_norms)


def solution(mesh):
    placed = (
        P(("ctg", "br")),
        P(("ctg", "br")),
        P("ctg", None, "br"),
        P("ctg", None, "br"),
        P("ctg", None, "br"),
        P("ctg", "br"),
        P("br"),
        P("br"),
        P("ctg", "br"),
        P("br"),
        P("br"),
        P("br"),
        P("br"),
        P("ctg", "br"),
        P("ctg", "br"),
    )
    return jax.shard_map(
        per_device,
        mesh=mesh,
        in_specs=placed,
        out_specs=(P("ctg", None, "br"), P("ctg", "br"), P("ctg", "br"), P("ctg", None), P()),
        check_vma=False,
    )
```

profile of v0, /device:TPU:0, one launch (start us, length us, event | category | flops | bytes accessed | tf_op | source)
XLA Modules:
  0.0 480.9 jit_solution(18033969470416528919)
XLA Ops:
  10.7 19.8 %all_gather.27 = f32[8,2,10240]{2,0,1:T(8,128)S(1)} all-gather(f32[8,2,2560]{2,0,1:T(8,128)S(1)} %copy.26), channel_id=1, replica_groups=mesh['ctg'=8,'br'=4] {'br'}, dimensions={2}, use_global_device_ids=true | all-gather | bytes 819200 | tf_op jit(solution)/shard_map/all_gather | solution.py:120
  30.6 16.5 %all_gather.29 = f32[8,2,10240]{2,0,1:T(8,128)S(1)} all-gather(f32[8,2,2560]{2,0,1:T(8,128)S(1)} %copy.27), channel_id=1, replica_groups=mesh['ctg'=8,'br'=4] {'br'}, dimensions={2}, use_global_device_ids=true | all-gather | bytes 819200 | tf_op jit(solution)/shard_map/all_gather | solution.py:121
  47.3 92.3 %all-reduce.6.cloned.1.call-done = (f32[10240]{0:T(1024)}, f32[10240]{0:T(1024)}) async-done(((f32[10240]{0:T(1024)}, f32[10240]{0:T(1024)}), (f32[10240]{0:T(1024)}, f32[10240]{0:T(1024)})) %all-reduce.6.cloned.1.call-update) | async-done | bytes 81936
  141.4 57.5 %while.34 = (s32[]{:T(128)}, f32[32,3328]{1,0:T(8,128)S(1)}, f32[10,32,1024]{2,1,0:T(8,128)S(1)}, s32[10]{0:T(128)S(1)}, s32[3328]{0:T(1024)S(1)}, /*index=5*/s32[]{:T(128)}, s32[1]{0:T(128)}, s32[]{:T(128)}) while((s32[]{:T(128)}, f32[32,3328]{1,0:T(8,128)S(1)}, f32[10,32,1024]{2,1,0:T(8,128)S(1)}, s32[10]{0:T(128)S(1)}, ...), condition=%wide.region_3.4_spmd.clone, body=%wide.region_2.3_spmd.clone.sunk | while | flops 1312244736 | bytes 1007743 | solution.py:32
  142.7 4.5 fusion.70
  159.9 4.5 fusion.70
  177.2 4.5 fusion.70
  199.0 57.5 %while.33 = (s32[]{:T(128)}, f32[32,3328]{1,0:T(8,128)S(1)}, f32[10,32,1024]{2,1,0:T(8,128)S(1)}, s32[10]{0:T(128)S(1)}, s32[3328]{0:T(1024)S(1)}, /*index=5*/s32[]{:T(128)}, s32[1]{0:T(128)}, s32[]{:T(128)}) while((s32[]{:T(128)}, f32[32,3328]{1,0:T(8,128)S(1)}, f32[10,32,1024]{2,1,0:T(8,128)S(1)}, s32[10]{0:T(128)S(1)}, ...), condition=%wide.region_1.2_spmd.clone, body=%wide.region_0.1_spmd.clone.sunk | while | flops 1312244736 | bytes 1007743 | solution.py:32
  258.8 14.7 %all-gather = s32[4,1,3328]{2,1,0:T(1,128)S(1)} all-gather(s32[1,1,3328]{2,1,0:T(1,128)S(1)} %reshape.69), channel_id=1, replica_groups=mesh['ctg'=8,'br'=4] {'br'}, dimensions={0}, use_global_device_ids=true | all-gather | bytes 66560 | tf_op jit(solution)/shard_map/all_gather | solution.py:152
  273.5 14.6 %all-gather.1 = s32[4,1,3328]{2,1,0:T(1,128)S(1)} all-gather(s32[1,1,3328]{2,1,0:T(1,128)S(1)} %reshape.71), channel_id=1, replica_groups=mesh['ctg'=8,'br'=4] {'br'}, dimensions={0}, use_global_device_ids=true | all-gather | bytes 66560 | tf_op jit(solution)/shard_map/all_gather | solution.py:153
  293.2 32.5 %all-gather.7.cloned.1.call-done = f32[8,3,13312]{2,0,1:T(8,128)} async-done(((f32[8,3,3328]{2,0,1:T(8,128)}), f32[8,3,13312]{2,0,1:T(8,128)}) %all-gather.7.cloned.1.call-update) | async-done | bytes 1277968 | tf_op jit(solution)/shard_map/all_gather | solution.py:149
  332.1 116.5 %while.32 = (s32[]{:T(128)}, f32[10,24,256]{2,1,0:T(8,128)}, s32[26624]{0:T(1024)S(1)}, s32[10]{0:T(128)S(1)}, f32[24,26624]{1,0:T(8,128)}, /*index=5*/s32[]{:T(128)}, s32[1]{0:T(128)}) while((s32[]{:T(128)}, f32[10,24,256]{2,1,0:T(8,128)}, s32[26624]{0:T(1024)S(1)}, s32[10]{0:T(128)S(1)}, f32[24,26624]{1,0:T(8,128)}, /*index=5*/s32[]{:T(128)}, ...), condition=%wide.region_5.6_spmd, body=%wide.region_4.5_spmd.sunk | while | flops 1969750272 | bytes 2689641 | solution.py:50
  333.4 10.4 %fusion.64 = f32[10,24,256]{2,1,0:T(8,128)} fusion(f32[10,24,256]{2,1,0:T(8,128)} %get-tuple-element.341, s32[]{:T(128)} %get-tuple-element.340, f32[24,26624]{1,0:T(8,128)} %get-tuple-element.351, s32[256]{0:T(256)S(1)} %iota_add_fusion.6, s32[26624]{0:T(1024)S(1)} %get-tuple-element.349), kind=kOutput, calls=%fused_computation.5.clone.1 | convolution fusion | flops 1969750016 | bytes 2688512 | tf_op jit(solution)/shard_map/while/body/eval_jaxpr/dot_general | solution.py:44
  345.0 10.4 %fusion.64 = f32[10,24,256]{2,1,0:T(8,128)} fusion(f32[10,24,256]{2,1,0:T(8,128)} %get-tuple-element.341, s32[]{:T(128)} %get-tuple-element.340, f32[24,26624]{1,0:T(8,128)} %get-tuple-element.351, s32[256]{0:T(256)S(1)} %iota_add_fusion.6, s32[26624]{0:T(1024)S(1)} %get-tuple-element.349), kind=kOutput, calls=%fused_computation.5.clone.1 | convolution fusion | flops 1969750016 | bytes 2688512 | tf_op jit(solution)/shard_map/while/body/eval_jaxpr/dot_general | solution.py:44
  356.7 10.4 %fusion.64 = f32[10,24,256]{2,1,0:T(8,128)} fusion(f32[10,24,256]{2,1,0:T(8,128)} %get-tuple-element.341, s32[]{:T(128)} %get-tuple-element.340, f32[24,26624]{1,0:T(8,128)} %get-tuple-element.351, s32[256]{0:T(256)S(1)} %iota_add_fusion.6, s32[26624]{0:T(1024)S(1)} %get-tuple-element.349), kind=kOutput, calls=%fused_computation.5.clone.1 | convolution fusion | flops 1969750016 | bytes 2688512 | tf_op jit(solution)/shard_map/while/body/eval_jaxpr/dot_general | solution.py:44
  368.3 10.4 %fusion.64 = f32[10,24,256]{2,1,0:T(8,128)} fusion(f32[10,24,256]{2,1,0:T(8,128)} %get-tuple-element.341, s32[]{:T(128)} %get-tuple-element.340, f32[24,26624]{1,0:T(8,128)} %get-tuple-element.351, s32[256]{0:T(256)S(1)} %iota_add_fusion.6, s32[26624]{0:T(1024)S(1)} %get-tuple-element.349), kind=kOutput, calls=%fused_computation.5.clone.1 | convolution fusion | flops 1969750016 | bytes 2688512 | tf_op jit(solution)/shard_map/while/body/eval_jaxpr/dot_general | solution.py:44
  380.0 10.4 %fusion.64 = f32[10,24,256]{2,1,0:T(8,128)} fusion(f32[10,24,256]{2,1,0:T(8,128)} %get-tuple-element.341, s32[]{:T(128)} %get-tuple-element.340, f32[24,26624]{1,0:T(8,128)} %get-tuple-element.351, s32[256]{0:T(256)S(1)} %iota_add_fusion.6, s32[26624]{0:T(1024)S(1)} %get-tuple-element.349), kind=kOutput, calls=%fused_computation.5.clone.1 | convolution fusion | flops 1969750016 | bytes 2688512 | tf_op jit(solution)/shard_map/while/body/eval_jaxpr/dot_general | solution.py:44
  391.6 10.4 %fusion.64 = f32[10,24,256]{2,1,0:T(8,128)} fusion(f32[10,24,256]{2,1,0:T(8,128)} %get-tuple-element.341, s32[]{:T(128)} %get-tuple-element.340, f32[24,26624]{1,0:T(8,128)} %get-tuple-element.351, s32[256]{0:T(256)S(1)} %iota_add_fusion.6, s32[26624]{0:T(1024)S(1)} %get-tuple-element.349), kind=kOutput, calls=%fused_computation.5.clone.1 | convolution fusion | flops 1969750016 | bytes 2688512 | tf_op jit(solution)/shard_map/while/body/eval_jaxpr/dot_general | solution.py:44
  403.2 10.4 %fusion.64 = f32[10,24,256]{2,1,0:T(8,128)} fusion(f32[10,24,256]{2,1,0:T(8,128)} %get-tuple-element.341, s32[]{:T(128)} %get-tuple-element.340, f32[24,26624]{1,0:T(8,128)} %get-tuple-element.351, s32[256]{0:T(256)S(1)} %iota_add_fusion.6, s32[26624]{0:T(1024)S(1)} %get-tuple-element.349), kind=kOutput, calls=%fused_computation.5.clone.1 | convolution fusion | flops 1969750016 | bytes 2688512 | tf_op jit(solution)/shard_map/while/body/eval_jaxpr/dot_general | solution.py:44
  414.9 10.4 %fusion.64 = f32[10,24,256]{2,1,0:T(8,128)} fusion(f32[10,24,256]{2,1,0:T(8,128)} %get-tuple-element.341, s32[]{:T(128)} %get-tuple-element.340, f32[24,26624]{1,0:T(8,128)} %get-tuple-element.351, s32[256]{0:T(256)S(1)} %iota_add_fusion.6, s32[26624]{0:T(1024)S(1)} %get-tuple-element.349), kind=kOutput, calls=%fused_computation.5.clone.1 | convolution fusion | flops 1969750016 | bytes 2688512 | tf_op jit(solution)/shard_map/while/body/eval_jaxpr/dot_general | solution.py:44
  426.6 10.4 %fusion.64 = f32[10,24,256]{2,1,0:T(8,128)} fusion(f32[10,24,256]{2,1,0:T(8,128)} %get-tuple-element.341, s32[]{:T(128)} %get-tuple-element.340, f32[24,26624]{1,0:T(8,128)} %get-tuple-element.351, s32[256]{0:T(256)S(1)} %iota_add_fusion.6, s32[26624]{0:T(1024)S(1)} %get-tuple-element.349), kind=kOutput, calls=%fused_computation.5.clone.1 | convolution fusion | flops 1969750016 | bytes 2688512 | tf_op jit(solution)/shard_map/while/body/eval_jaxpr/dot_general | solution.py:44
  438.2 10.4 %fusion.64 = f32[10,24,256]{2,1,0:T(8,128)} fusion(f32[10,24,256]{2,1,0:T(8,128)} %get-tuple-element.341, s32[]{:T(128)} %get-tuple-element.340, f32[24,26624]{1,0:T(8,128)} %get-tuple-element.351, s32[256]{0:T(256)S(1)} %iota_add_fusion.6, s32[26624]{0:T(1024)S(1)} %get-tuple-element.349), kind=kOutput, calls=%fused_computation.5.clone.1 | convolution fusion | flops 1969750016 | bytes 2688512 | tf_op jit(solution)/shard_map/while/body/eval_jaxpr/dot_general | solution.py:44
  451.4 10.0 %all-reduce.3 = (f32[8,1]{0,1:T(1,128)S(1)}, f32[8,1]{0,1:T(1,128)S(1)}, f32[8,1]{0,1:T(1,128)S(1)}, f32[8,1]{0,1:T(1,128)S(1)}) all-reduce(f32[8,1]{0,1:T(1,128)S(1)} %bitcast.75, f32[8,1]{0,1:T(1,128)S(1)} %bitcast.74, f32[8,1]{0,1:T(1,128)S(1)} %bitcast.77, f32[8,1]{0,1:T(1,128)S(1)} %bitcast.76), channel_id=1, replica_groups=mesh['ctg'=8,'br'=4] {'br'}, use_global_device_ids=true, to_apply=%region_13.14 | all-reduce | flops 32 | bytes 256 | tf_op jit(solution)/shard_map/psum | solution.py:146
  462.1 11.8 %psum.39 = f32[4]{0:T(128)S(1)} all-reduce(f32[4]{0:T(128)S(1)} %get-tuple-element.188), channel_id=1, replica_groups=mesh['ctg'=8,'br'=4] {'ctg'}, use_global_device_ids=true, to_apply=%region_15.16 | all-reduce | flops 4 | bytes 32 | tf_op jit(solution)/shard_map/psum | solution.py:163
  (150 shorter events, 116.8 us)
Async XLA Ops:
  7.2 23.4 %copy-start.1 = (f32[8,2,2560]{2,1,0:T(2,128)S(1)}, f32[8,2,2560]{2,1,0:T(2,128)}, u32[]{:S(2)}) copy-start(f32[8,2,2560]{2,1,0:T(2,128)} %param.24) | copy-start | bytes 491524
  7.2 40.0 %copy-start.5 = (f32[3328]{0:T(1024)S(1)}, f32[3328]{0:T(1024)}, u32[]{:S(2)}) copy-start(f32[3328]{0:T(1024)} %param.31) | copy-start | bytes 39940
  7.2 40.0 %copy-start.11 = (f32[3328]{0:T(1024)S(1)}, f32[3328]{0:T(1024)}, u32[]{:S(2)}) copy-start(f32[3328]{0:T(1024)} %param.32) | copy-start | bytes 39940
  7.2 132.4 %all-reduce.6.cloned.1.call-start = ((), (), s32[]{:S(2)}) async-start(), calls=%async_computation.2 | async-start | bytes 163840
  7.3 40.0 %copy-start = (s32[8,3328]{1,0:T(8,128)S(1)}, s32[8,3328]{1,0:T(8,128)}, u32[]{:S(2)}) copy-start(s32[8,3328]{1,0:T(8,128)} %param.29) | copy-start | bytes 319492
  8.2 0.9 copy-start.4
  9.1 0.6 copy-start.3
  9.7 283.4 %all-gather.5.cloned.1.call-start = ((), (), s32[]{:S(2)}) async-start(), calls=%async_computation | async-start | bytes 1597440 | tf_op jit(solution)/shard_map/all_gather | solution.py:148
  47.2 94.2 %copy-start.13 = (s32[3328]{0:T(1024)S(1)}, s32[3328]{0:T(1024)}, u32[]{:S(2)}) copy-start(s32[3328]{0:T(1024)} %param.28) | copy-start | bytes 39940
  141.4 57.5 %copy-start.12 = (s32[3328]{0:T(1024)S(1)}, s32[3328]{0:T(1024)}, u32[]{:S(2)}) copy-start(s32[3328]{0:T(1024)} %param.27) | copy-start | bytes 39940
  198.9 57.5 %copy-start.9 = (f32[3328]{0:T(1024)S(1)}, f32[3328]{0:T(1024)}, u32[]{:S(2)}) copy-start(f32[3328]{0:T(1024)} %param.30) | copy-start | bytes 39940
  256.5 2.3 copy-start.10
  256.5 31.6 %copy-start.6 = (f32[8,3328]{1,0:T(8,128)S(1)}, f32[8,3328]{1,0:T(8,128)}, u32[]{:S(2)}) copy-start(f32[8,3328]{1,0:T(8,128)} %param.34) | copy-start | bytes 319492
  256.5 31.6 %copy-start.7 = (f32[8,3328]{1,0:T(8,128)S(1)}, f32[8,3328]{1,0:T(8,128)}, u32[]{:S(2)}) copy-start(f32[8,3328]{1,0:T(8,128)} %param.35) | copy-start | bytes 319492
  258.0 67.8 %all-gather.7.cloned.1.call-start = ((), (), s32[]{:S(2)}) async-start(), calls=%async_computation.1 | async-start | bytes 1597440 | tf_op jit(solution)/shard_map/all_gather | solution.py:149
  332.1 117.8 %copy-start.2 = (f32[8,2,2560]{2,1,0:T(2,128)S(1)}, f32[8,2,2560]{2,1,0:T(2,128)}, u32[]{:S(2)}) copy-start(f32[8,2,2560]{2,1,0:T(2,128)} %param.25) | copy-start | bytes 491524
  332.1 118.6 %copy-start.8 = (f32[8,2560]{1,0:T(8,128)S(1)}, f32[8,2560]{1,0:T(8,128)}, u32[]{:S(2)}) copy-start(f32[8,2560]{1,0:T(8,128)} %param.26) | copy-start | bytes 245764
Sparse Core Ops, SparseCore 0:
  14.2 125.3 all-reduce.5
  258.1 35.0 all-gather.4
  294.8 30.9 all-gather.6
where the time goes:
time: 482 us; the launch traced here: 481 us
  matrix products  193 us (40%)
  waiting for transfers between devices  129 us (27%)
  blocking collectives  87.4 us (18%)
  local copies, waits for them, and re-layouts  28.5 us (6%)
  loops' own time  20.3 us (4%)
  between operations  14.1 us (3%)
  other arithmetic  8.15 us (2%)
    dot_general x10, matrix products, one_block(): jnp.dot(values, onehot, precision=lax.Precision.HIGHEST, preferred_elemen...  104 us
    unnamed x4, waiting for transfers between devices  93.1 us
    dot_general x20, matrix products, add_block(): jnp.dot(segment, onehot, precision=lax.Precision.HIGHEST, preferred_eleme...  89.4 us
    all_gather x1, waiting for transfers between devices, per_device(): lax.all_gather(at_to, 'br', axis=2, tiled=True)  32.5 us
    all_gather x1, blocking collectives, per_device(): lax.all_gather(delta_state, 'br', axis=2, tiled=True)  19.8 us
    dynamic_slice x30, local copies, waits for them, and re-layouts, select_cols(): result, _ = lax.scan(add_block, start_zero, (tiles, numbers))  17.5 us
    all_gather x1, blocking collectives, per_device(): lax.all_gather(multipliers, 'br', axis=2, tiled=True)  16.5 us
    all_gather x1, blocking collectives, per_device(): lax.all_gather(from_bus, 'br', axis=0, tiled=True)  14.7 us
  transfers between devices with their start and end apart: 3, of which 3 were waited for; matrix products, arithmetic and copies ran while one was open for 1% of the time, Pallas kernels for 0%

commit v1 on v0

--- a/solution.py
+++ b/solution.py
@@ -3,6 +3,7 @@
 import jax.numpy as jnp
 from jax import lax
 from jax.sharding import PartitionSpec as P
+from jax.lax import all_gather
 
 
 def block_size(span_total, other_side):
@@ -146,7 +147,7 @@
     limit_sq, comp_sq = lax.psum((limit_part, comp_part), "br")
     every_from, every_to = (
         lax.all_gather(at_from, "br", axis=2, tiled=True),
-        lax.all_gather(at_to, "br", axis=2, tiled=True),
+        jnp.concatenate(all_gather(at_to, axis_name="br"), axis=2),
     )
     ends_from, ends_to = (
         lax.all_gather(from_bus, "br", axis=0, tiled=True),

time: 482 us -> 473 us (0.981)
  matrix products: 193 us -> 187 us
    dot_general x10, matrix products: 104 us -> 97.9 us  [one_block(): jnp.dot(values, onehot, precision=lax.Precision.HIGHEST, preferred_elemen...]
where the time goes in v1:
time: 473 us; the launch traced here: 472 us
  matrix products  187 us (40%)
  waiting for transfers between devices  126 us (27%)
  blocking collectives  87.3 us (18%)
  local copies, waits for them, and re-layouts  28.4 us (6%)
  loops' own time  20.3 us (4%)
  between operations  14.1 us (3%)
  other arithmetic  7.7 us (2%)
    dot_general x10, matrix products, one_block(): jnp.dot(values, onehot, precision=lax.Precision.HIGHEST, preferred_elemen...  97.9 us
    unnamed x4, waiting for transfers between devices  92.4 us
    dot_general x20, matrix products, add_block(): jnp.dot(segment, onehot, precision=lax.Precision.HIGHEST, preferred_eleme...  89.5 us
    all_gather x1, waiting for transfers between devices, per_device(): all_gather(at_to, axis_name='br')  29.7 us
    all_gather x1, blocking collectives, per_device(): lax.all_gather(delta_state, 'br', axis=2, tiled=True)  19.8 us
    dynamic_slice x30, local copies, waits for them, and re-layouts, select_cols(): result, _ = lax.scan(add_block, start_zero, (tiles, numbers))  17.6 us
    all_gather x1, blocking collectives, per_device(): lax.all_gather(multipliers, 'br', axis=2, tiled=True)  16.5 us
    all_gather x1, blocking collectives, per_device(): lax.all_gather(from_bus, 'br', axis=0, tiled=True)  14.7 us
  transfers between devices with their start and end apart: 3, of which 3 were waited for; matrix products, arithmetic and copies ran while one was open for 1% of the time, Pallas kernels for 0%

profile of v1, /device:TPU:0, one launch (start us, length us, event | category | flops | bytes accessed | tf_op | source)
XLA Modules:
  0.0 471.5 jit_solution(5529265967075894320)
XLA Ops:
  10.7 19.8 %all_gather.28 = f32[8,2,10240]{2,0,1:T(8,128)S(1)} all-gather(f32[8,2,2560]{2,0,1:T(8,128)S(1)} %copy.27), channel_id=1, replica_groups=mesh['ctg'=8,'br'=4] {'br'}, dimensions={2}, use_global_device_ids=true | all-gather | bytes 819200 | tf_op jit(solution)/shard_map/all_gather | solution.py:121
  30.6 16.5 %all_gather.30 = f32[8,2,10240]{2,0,1:T(8,128)S(1)} all-gather(f32[8,2,2560]{2,0,1:T(8,128)S(1)} %copy.28), channel_id=1, replica_groups=mesh['ctg'=8,'br'=4] {'br'}, dimensions={2}, use_global_device_ids=true | all-gather | bytes 819200 | tf_op jit(solution)/shard_map/all_gather | solution.py:122
  47.2 92.3 %all-reduce.6.cloned.1.call-done = (f32[10240]{0:T(1024)}, f32[10240]{0:T(1024)}) async-done(((f32[10240]{0:T(1024)}, f32[10240]{0:T(1024)}), (f32[10240]{0:T(1024)}, f32[10240]{0:T(1024)})) %all-reduce.6.cloned.1.call-update) | async-done | bytes 81936
  141.8 57.5 %while.34 = (s32[]{:T(128)}, f32[32,3328]{1,0:T(8,128)S(1)}, f32[10,32,1024]{2,1,0:T(8,128)S(1)}, s32[10]{0:T(128)S(1)}, s32[3328]{0:T(1024)S(1)}, /*index=5*/s32[]{:T(128)}, s32[1]{0:T(128)}, s32[]{:T(128)}) while((s32[]{:T(128)}, f32[32,3328]{1,0:T(8,128)S(1)}, f32[10,32,1024]{2,1,0:T(8,128)S(1)}, s32[10]{0:T(128)S(1)}, ...), condition=%wide.region_3.4_spmd.clone, body=%wide.region_2.3_spmd.clone.sunk | while | flops 1312244736 | bytes 1007743 | solution.py:33
  199.3 57.5 %while.33 = (s32[]{:T(128)}, f32[32,3328]{1,0:T(8,128)S(1)}, f32[10,32,1024]{2,1,0:T(8,128)S(1)}, s32[10]{0:T(128)S(1)}, s32[3328]{0:T(1024)S(1)}, /*index=5*/s32[]{:T(128)}, s32[1]{0:T(128)}, s32[]{:T(128)}) while((s32[]{:T(128)}, f32[32,3328]{1,0:T(8,128)S(1)}, f32[10,32,1024]{2,1,0:T(8,128)S(1)}, s32[10]{0:T(128)S(1)}, ...), condition=%wide.region_1.2_spmd.clone, body=%wide.region_0.1_spmd.clone.sunk | while | flops 1312244736 | bytes 1007743 | solution.py:33
  200.6 4.5 fusion.67
  206.4 4.5 fusion.67
  212.1 4.5 fusion.67
  259.2 14.7 %all-gather = s32[4,1,3328]{2,1,0:T(1,128)S(1)} all-gather(s32[1,1,3328]{2,1,0:T(1,128)S(1)} %reshape.119), channel_id=1, replica_groups=mesh['ctg'=8,'br'=4] {'br'}, dimensions={0}, use_global_device_ids=true | all-gather | bytes 66560 | tf_op jit(solution)/shard_map/all_gather | solution.py:153
  273.9 14.5 %all-gather.1 = s32[4,1,3328]{2,1,0:T(1,128)S(1)} all-gather(s32[1,1,3328]{2,1,0:T(1,128)S(1)} %reshape.121), channel_id=1, replica_groups=mesh['ctg'=8,'br'=4] {'br'}, dimensions={0}, use_global_device_ids=true | all-gather | bytes 66560 | tf_op jit(solution)/shard_map/all_gather | solution.py:154
  296.3 29.7 %all-gather.7.cloned.1.call-done = f32[4,8,3,3328]{3,1,2,0:T(8,128)} async-done(((f32[1,8,3,3328]{3,1,2,0:T(8,128)}), f32[4,8,3,3328]{3,1,2,0:T(8,128)}) %all-gather.7.cloned.1.call-update) | async-done | bytes 1277968 | tf_op jit(solution)/shard_map/all_gather | solution.py:150
  329.7 110.4 %while.32 = (s32[]{:T(128)}, f32[10,24,256]{2,1,0:T(8,128)S(1)}, s32[26624]{0:T(1024)S(1)}, s32[10]{0:T(128)S(1)}, f32[24,26624]{1,0:T(8,128)}, /*index=5*/s32[]{:T(128)}, s32[1]{0:T(128)}) while((s32[]{:T(128)}, f32[10,24,256]{2,1,0:T(8,128)S(1)}, s32[26624]{0:T(1024)S(1)}, s32[10]{0:T(128)S(1)}, f32[24,26624]{1,0:T(8,128)}, ...), condition=%wide.region_5.6_spmd, body=%wide.region_4.5_spmd.sunk | while | flops 1969750272 | bytes 2689133 | solution.py:51
  331.0 9.8 %fusion.64 = f32[10,24,256]{2,1,0:T(8,128)S(1)} fusion(f32[10,24,256]{2,1,0:T(8,128)S(1)} %get-tuple-element.339, s32[]{:T(128)} %get-tuple-element.338, f32[24,26624]{1,0:T(8,128)} %get-tuple-element.349, s32[256]{0:T(256)S(1)} %iota_add_fusion.6, s32[26624]{0:T(1024)S(1)} %get-tuple-element.347), kind=kOutput, calls=%fused_computation.5.clone.1 | convolution fusion | flops 1969750016 | bytes 2688004 | tf_op jit(solution)/shard_map/while/body/eval_jaxpr/dot_general | solution.py:45
  342.0 9.8 %fusion.64 = f32[10,24,256]{2,1,0:T(8,128)S(1)} fusion(f32[10,24,256]{2,1,0:T(8,128)S(1)} %get-tuple-element.339, s32[]{:T(128)} %get-tuple-element.338, f32[24,26624]{1,0:T(8,128)} %get-tuple-element.349, s32[256]{0:T(256)S(1)} %iota_add_fusion.6, s32[26624]{0:T(1024)S(1)} %get-tuple-element.347), kind=kOutput, calls=%fused_computation.5.clone.1 | convolution fusion | flops 1969750016 | bytes 2688004 | tf_op jit(solution)/shard_map/while/body/eval_jaxpr/dot_general | solution.py:45
  353.1 9.8 %fusion.64 = f32[10,24,256]{2,1,0:T(8,128)S(1)} fusion(f32[10,24,256]{2,1,0:T(8,128)S(1)} %get-tuple-element.339, s32[]{:T(128)} %get-tuple-element.338, f32[24,26624]{1,0:T(8,128)} %get-tuple-element.349, s32[256]{0:T(256)S(1)} %iota_add_fusion.6, s32[26624]{0:T(1024)S(1)} %get-tuple-element.347), kind=kOutput, calls=%fused_computation.5.clone.1 | convolution fusion | flops 1969750016 | bytes 2688004 | tf_op jit(solution)/shard_map/while/body/eval_jaxpr/dot_general | solution.py:45
  364.1 9.8 %fusion.64 = f32[10,24,256]{2,1,0:T(8,128)S(1)} fusion(f32[10,24,256]{2,1,0:T(8,128)S(1)} %get-tuple-element.339, s32[]{:T(128)} %get-tuple-element.338, f32[24,26624]{1,0:T(8,128)} %get-tuple-element.349, s32[256]{0:T(256)S(1)} %iota_add_fusion.6, s32[26624]{0:T(1024)S(1)} %get-tuple-element.347), kind=kOutput, calls=%fused_computation.5.clone.1 | convolution fusion | flops 1969750016 | bytes 2688004 | tf_op jit(solution)/shard_map/while/body/eval_jaxpr/dot_general | solution.py:45
  375.1 9.8 %fusion.64 = f32[10,24,256]{2,1,0:T(8,128)S(1)} fusion(f32[10,24,256]{2,1,0:T(8,128)S(1)} %get-tuple-element.339, s32[]{:T(128)} %get-tuple-element.338, f32[24,26624]{1,0:T(8,128)} %get-tuple-element.349, s32[256]{0:T(256)S(1)} %iota_add_fusion.6, s32[26624]{0:T(1024)S(1)} %get-tuple-element.347), kind=kOutput, calls=%fused_computation.5.clone.1 | convolution fusion | flops 1969750016 | bytes 2688004 | tf_op jit(solution)/shard_map/while/body/eval_jaxpr/dot_general | solution.py:45
  386.2 9.8 %fusion.64 = f32[10,24,256]{2,1,0:T(8,128)S(1)} fusion(f32[10,24,256]{2,1,0:T(8,128)S(1)} %get-tuple-element.339, s32[]{:T(128)} %get-tuple-element.338, f32[24,26624]{1,0:T(8,128)} %get-tuple-element.349, s32[256]{0:T(256)S(1)} %iota_add_fusion.6, s32[26624]{0:T(1024)S(1)} %get-tuple-element.347), kind=kOutput, calls=%fused_computation.5.clone.1 | convolution fusion | flops 1969750016 | bytes 2688004 | tf_op jit(solution)/shard_map/while/body/eval_jaxpr/dot_general | solution.py:45
  397.2 9.8 %fusion.64 = f32[10,24,256]{2,1,0:T(8,128)S(1)} fusion(f32[10,24,256]{2,1,0:T(8,128)S(1)} %get-tuple-element.339, s32[]{:T(128)} %get-tuple-element.338, f32[24,26624]{1,0:T(8,128)} %get-tuple-element.349, s32[256]{0:T(256)S(1)} %iota_add_fusion.6, s32[26624]{0:T(1024)S(1)} %get-tuple-element.347), kind=kOutput, calls=%fused_computation.5.clone.1 | convolution fusion | flops 1969750016 | bytes 2688004 | tf_op jit(solution)/shard_map/while/body/eval_jaxpr/dot_general | solution.py:45
  408.3 9.8 %fusion.64 = f32[10,24,256]{2,1,0:T(8,128)S(1)} fusion(f32[10,24,256]{2,1,0:T(8,128)S(1)} %get-tuple-element.339, s32[]{:T(128)} %get-tuple-element.338, f32[24,26624]{1,0:T(8,128)} %get-tuple-element.349, s32[256]{0:T(256)S(1)} %iota_add_fusion.6, s32[26624]{0:T(1024)S(1)} %get-tuple-element.347), kind=kOutput, calls=%fused_computation.5.clone.1 | convolution fusion | flops 1969750016 | bytes 2688004 | tf_op jit(solution)/shard_map/while/body/eval_jaxpr/dot_general | solution.py:45
  419.3 9.8 %fusion.64 = f32[10,24,256]{2,1,0:T(8,128)S(1)} fusion(f32[10,24,256]{2,1,0:T(8,128)S(1)} %get-tuple-element.339, s32[]{:T(128)} %get-tuple-element.338, f32[24,26624]{1,0:T(8,128)} %get-tuple-element.349, s32[256]{0:T(256)S(1)} %iota_add_fusion.6, s32[26624]{0:T(1024)S(1)} %get-tuple-element.347), kind=kOutput, calls=%fused_computation.5.clone.1 | convolution fusion | flops 1969750016 | bytes 2688004 | tf_op jit(solution)/shard_map/while/body/eval_jaxpr/dot_general | solution.py:45
  430.3 9.8 %fusion.64 = f32[10,24,256]{2,1,0:T(8,128)S(1)} fusion(f32[10,24,256]{2,1,0:T(8,128)S(1)} %get-tuple-element.339, s32[]{:T(128)} %get-tuple-element.338, f32[24,26624]{1,0:T(8,128)} %get-tuple-element.349, s32[256]{0:T(256)S(1)} %iota_add_fusion.6, s32[26624]{0:T(1024)S(1)} %get-tuple-element.347), kind=kOutput, calls=%fused_computation.5.clone.1 | convolution fusion | flops 1969750016 | bytes 2688004 | tf_op jit(solution)/shard_map/while/body/eval_jaxpr/dot_general | solution.py:45
  442.0 10.0 %all-reduce.3 = (f32[8,1]{0,1:T(1,128)S(1)}, f32[8,1]{0,1:T(1,128)S(1)}, f32[8,1]{0,1:T(1,128)S(1)}, f32[8,1]{0,1:T(1,128)S(1)}) all-reduce(f32[8,1]{0,1:T(1,128)S(1)} %bitcast.82, f32[8,1]{0,1:T(1,128)S(1)} %bitcast.81, f32[8,1]{0,1:T(1,128)S(1)} %bitcast.84, f32[8,1]{0,1:T(1,128)S(1)} %bitcast.83), channel_id=1, replica_groups=mesh['ctg'=8,'br'=4] {'br'}, use_global_device_ids=true, to_apply=%region_13.14 | all-reduce | flops 32 | bytes 256 | tf_op jit(solution)/shard_map/psum | solution.py:147
  452.7 11.8 %psum.39 = f32[4]{0:T(128)S(1)} all-reduce(f32[4]{0:T(128)S(1)} %get-tuple-element.186), channel_id=1, replica_groups=mesh['ctg'=8,'br'=4] {'ctg'}, use_global_device_ids=true, to_apply=%region_15.16 | all-reduce | flops 4 | bytes 32 | tf_op jit(solution)/shard_map/psum | solution.py:164
  (155 shorter events, 116.4 us)
Async XLA Ops:
  7.2 23.4 %copy-start.2 = (f32[8,2,2560]{2,1,0:T(2,128)S(1)}, f32[8,2,2560]{2,1,0:T(2,128)}, u32[]{:S(2)}) copy-start(f32[8,2,2560]{2,1,0:T(2,128)} %param.24) | copy-start | bytes 491524
  7.2 132.3 %all-reduce.6.cloned.1.call-start = ((), (), s32[]{:S(2)}) async-start(), calls=%async_computation.2 | async-start | bytes 163840
  8.1 0.9 copy-start.5
  9.0 0.6 copy-start.4
  9.7 283.8 %all-gather.5.cloned.1.call-start = ((), (), s32[]{:S(2)}) async-start(), calls=%async_computation | async-start | bytes 1597440 | tf_op jit(solution)/shard_map/all_gather | solution.py:149
  30.5 16.6 %copy-start.6 = (f32[3328]{0:T(1024)S(1)}, f32[3328]{0:T(1024)}, u32[]{:S(2)}) copy-start(f32[3328]{0:T(1024)} %param.31) | copy-start | bytes 39940
  30.5 16.6 %copy-start.12 = (f32[3328]{0:T(1024)S(1)}, f32[3328]{0:T(1024)}, u32[]{:S(2)}) copy-start(f32[3328]{0:T(1024)} %param.32) | copy-start | bytes 39940
  30.5 16.7 %copy-start.1 = (s32[8,3328]{1,0:T(8,128)S(1)}, s32[8,3328]{1,0:T(8,128)}, u32[]{:S(2)}) copy-start(s32[8,3328]{1,0:T(8,128)} %param.29) | copy-start | bytes 319492
  141.1 0.7 copy-start.14
  141.8 57.5 %copy-start.13 = (s32[3328]{0:T(1024)S(1)}, s32[3328]{0:T(1024)}, u32[]{:S(2)}) copy-start(s32[3328]{0:T(1024)} %param.27) | copy-start | bytes 39940
  199.3 57.5 %copy-start.10 = (f32[3328]{0:T(1024)S(1)}, f32[3328]{0:T(1024)}, u32[]{:S(2)}) copy-start(f32[3328]{0:T(1024)} %param.30) | copy-start | bytes 39940
  257.3 1.8 copy-start.11
  257.3 31.2 %copy-start.7 = (f32[8,3328]{1,0:T(8,128)S(1)}, f32[8,3328]{1,0:T(8,128)}, u32[]{:S(2)}) copy-start(f32[8,3328]{1,0:T(8,128)} %param.34) | copy-start | bytes 319492
  257.3 31.2 %copy-start.8 = (f32[8,3328]{1,0:T(8,128)S(1)}, f32[8,3328]{1,0:T(8,128)}, u32[]{:S(2)}) copy-start(f32[8,3328]{1,0:T(8,128)} %param.35) | copy-start | bytes 319492
  258.2 30.3 %copy-start = (f32[8,3,3328]{2,0,1:T(8,128)S(1)}, f32[8,3,3328]{2,0,1:T(8,128)}, u32[]{:S(2)}) copy-start(f32[8,3,3328]{2,0,1:T(8,128)} %maximum_multiply_fusion) | copy-start | bytes 958468
  258.2 67.8 %all-gather.7.cloned.1.call-start = ((), (), s32[]{:S(2)}) async-start(), calls=%async_computation.1 | async-start | bytes 1597440 | tf_op jit(solution)/shard_map/all_gather | solution.py:150
  329.7 110.8 %copy-start.3 = (f32[8,2,2560]{2,1,0:T(2,128)S(1)}, f32[8,2,2560]{2,1,0:T(2,128)}, u32[]{:S(2)}) copy-start(f32[8,2,2560]{2,1,0:T(2,128)} %param.25) | copy-start | bytes 491524
  440.1 1.1 copy-start.9
Sparse Core Ops, SparseCore 0:
  14.2 125.2 all-reduce.5
  258.4 35.0 all-gather.4
  295.1 30.9 all-gather.6
